TPU v7x, 32 devices: a whole 2x2x4 slice. The times are simulated.
32 devices in a mesh: group: 2 (over y), fsdp: 16 (over z, x, core).
Axes of the slice: x: 2, y: 2, z: 4, core: 2. Of those that a mesh axis runs over, the one named last changes fastest.
Arguments:
- teacher_rows: bfloat16 [20480, 2048], P(('group', 'fsdp')), may hold values from -6 to 6
- student_rows: bfloat16 [20480, 1024], P(('group', 'fsdp')), may hold values from -6 to 6
- counts: int32 [32], P(('group', 'fsdp')), may hold values from 213 to 640, as said below
- teacher_weight: bfloat16 [2048, 4096], P(None, ('group', 'fsdp')), may hold values from -0.125 to 0.125
- teacher_bias: float32 [4096], replicated, may hold values from -6 to 6
- teacher_gain: float32 [4096], replicated, may hold values from 0.1 to 1.9
- teacher_head: float32 [4096], replicated, may hold values from -0.09375 to 0.09375
- cross_weight: bfloat16 [1024, 1024], replicated, may hold values from -0.1875 to 0.1875
- cross_bias: float32 [1024], replicated, may hold values from -3 to 3
- out_weight: float32 [1024], replicated, may hold values from -0.1875 to 0.1875
Outputs:
- grad_cross: float32 [1024, 1024], P('fsdp')
- grad_bias: float32 [1024], replicated
- grad_out: float32 [1024], replicated
Inputs may be any that keep to these rules, and one draw needn't show every extreme that they name: counts[i] live impressions fill the first slots of shard i, the rest of its 640 slots are padding.
All inputs are finite; a program needn't handle non-finite values.
Results may differ from a plain program's by a relative error of at most 0.00035.
The roundings to bfloat16 on the way count: a program that leaves them out, or rounds other values in their place, can miss the bound.
Values may be sent and summed in bfloat16 or wider, within the bound.
A program may use at most 128 MiB of HBM per device.

v0:
```python
import functools
import math

import jax
import jax.numpy as jnp
from jax import lax
from jax.experimental import pallas as pl
from jax.experimental.pallas import tpu as pltpu
from jax.sharding import PartitionSpec as P

epsilon = 1e-06


def shards(
    teacher_rows,
    student_rows,
    counts,
    teacher_weight,
    teacher_bias,
    teacher_gain,
    teacher_head,
    cross_weight,
    cross_bias,
    out_weight,
):
    row_count = teacher_rows.shape[0]
    width_s = cross_weight.shape[0]
    group_count = lax.axis_size("group")
    fsdp_count = lax.axis_size("fsdp")
    shard_count = group_count * fsdp_count
    loss_scale = math.sqrt(width_s / (row_count * shard_count))
    preact = jnp.dot(
        teacher_rows,
        lax.all_gather(teacher_weight, ("group", "fsdp"), axis=1, tiled=True),
        preferred_element_type=jnp.float32,
    )
    preact = preact + teacher_bias
    meansq = jnp.mean(preact * preact, axis=-1, keepdims=True)
    normed = preact * lax.rsqrt(meansq + epsilon) * teacher_gain
    teacher_logit = jnp.sum(jax.nn.silu(normed) * teacher_head, axis=-1)
    cross = jnp.dot(student_rows, cross_weight, preferred_element_type=jnp.float32) + cross_bias
    inputs_f = student_rows.astype(jnp.float32)
    mixed = inputs_f * cross + inputs_f
    student_logit = jnp.sum(mixed * out_weight, axis=-1)
    live_rows = (jnp.arange(row_count, dtype=jnp.int32) < counts[0]).astype(jnp.float32)
    error = (student_logit - teacher_logit) * live_rows * loss_scale
    dcross = error[:, None] * out_weight[None, :] * inputs_f
    dcross_half = dcross.astype(jnp.bfloat16)
    term_b = jnp.sum(dcross, axis=0)
    term_o = jnp.sum(error[:, None] * mixed, axis=0)
    term_w = lax.dot_general(
        student_rows, dcross_half, (((0,), (0,)), ((), ())), preferred_element_type=jnp.float32
    )
    totals = lax.psum((term_w, term_b, term_o), "group")
    grad_cross = lax.psum_scatter(totals[0], "fsdp", scatter_dimension=0, tiled=True)
    small_sums = lax.psum((totals[1], totals[2]), "fsdp")
    return (grad_cross, small_sums[0], small_sums[1])


MESH = pl.DeviceIdType.MESH
LANES = 128
PAIRS = 4


def fused(fsdp_count, rp, t_ref, s_ref, live_ref, w_ref, bias_ref, gain_ref, head_ref, cw_ref, cb_ref, ow_ref,
          out_ref, small_ref,
          wbuf, rows, xs, cw, pre, ssq, gains, heads, mixed, msg1, in1, msg2, in2, rr, er, xt, dbuf,
          tw, r1, s1, r2, tt, r3, fin, r4, sb, rb, rz, lsem, ssem, rsem):
    g = lax.axis_index("group")
    f = lax.axis_index("fsdp")
    core = lax.rem(f, 2)
    x = lax.rem(lax.div(f, 2), 2)
    z = lax.div(f, 4)
    nz = fsdp_count // 4
    row_count, fin_width = t_ref.shape
    width_s = s_ref.shape[1]
    block = width_s // fsdp_count
    half_rows = block // 2
    rt = row_count // LANES
    units = bias_ref.shape[0] * LANES
    parts = 2 * PAIRS
    pw = width_s // parts

    def at(y_, z_, x_, c_):
        return (y_, (z_ * 2 + x_) * 2 + c_)

    partner = at(g, z, x, 1 - core)
    xn = at(g, z, 1 - x, core)
    yn = at(1 - g, z, x, core)
    barrier = pltpu.get_barrier_semaphore()
    peers = [partner, xn, yn] + [at(g, lax.rem(z + k, nz), x, core) for k in range(1, nz)]
    for peer in peers:
        pl.semaphore_signal(barrier, inc=1, device_id=peer, device_id_type=MESH)

    locals_ = []
    for i, (a, b) in enumerate([
        (s_ref, xs.at[pl.ds(0, row_count)]),
        (cw_ref, cw),
        (w_ref, wbuf.at[0]),
        (t_ref, rows.at[pl.ds(0, row_count)]),
    ]):
        cp = pltpu.make_async_copy(a, b, lsem.at[i])
        cp.start()
        locals_.append(cp)
    pl.semaphore_wait(barrier, len(peers))

    sends = []

    def send(a, b, device):
        i = len(sends)
        cp = pltpu.make_async_remote_copy(
            src_ref=a, dst_ref=b, send_sem=ssem.at[i], recv_sem=rsem.at[i], device_id=device, device_id_type=MESH
        )
        cp.start()
        sends.append(cp)
        return cp

    def slot(dx, dy, dz):
        return (dx * 2 + dy) * nz + dz

    order = [1] + list(range(nz - 1, 1, -1))
    depth = fin_width // 2
    xin, yin, zin, din = {}, {}, {}, {}

    def half(ref, h):
        return ref.at[pl.ds(h * depth, depth)]

    def piece(dx, dy, dz, h):
        return wbuf.at[slot(dx, dy, dz), pl.ds(h * depth, depth)]

    def zpeer(k):
        return at(g, lax.rem(z + nz - k, nz), x, core)

    for h in range(2):
        xin[0, h] = send(half(w_ref, h), piece(1, 0, 0, h), xn)
        yin[0, h] = send(half(w_ref, h), piece(0, 1, 0, h), yn)
        zin[order[0], h] = send(half(w_ref, h), piece(0, 0, order[0], h), zpeer(order[0]))
    for k in order[1:]:
        for h in range(2):
            zin[k, h] = send(half(w_ref, h), piece(0, 0, k, h), zpeer(k))
    rows_in = send(t_ref, rows.at[pl.ds(row_count, row_count)], partner)
    xs_in = send(s_ref, xs.at[pl.ds(row_count, row_count)], partner)

    def diagonal(k, h):
        lo, hi = pl.ds(h * depth, depth // 2), pl.ds(h * depth + depth // 2, depth // 2)
        xin[k, h].wait_recv()
        a = send(wbuf.at[slot(1, 0, k), lo], wbuf.at[slot(1, 1, k), lo], yn)
        yin[k, h].wait_recv()
        b = send(wbuf.at[slot(0, 1, k), hi], wbuf.at[slot(1, 1, k), hi], xn)
        din[k, h] = (a, b)

    def relay(k, h):
        zin[k, h].wait_recv()
        xin[k, h] = send(piece(0, 0, k, h), piece(1, 0, k, h), xn)
        yin[k, h] = send(piece(0, 0, k, h), piece(0, 1, k, h), yn)

    def arrived(k, h):
        for cp in din[k, h]:
            cp.wait_recv()

    def along(k, h):
        arrived(0, h)
        din[k, h] = (send(piece(1, 1, 0, h), piece(1, 1, k, h), zpeer(k)),)

    eye = lax.broadcasted_iota(jnp.int32, (LANES, LANES), 0) == lax.broadcasted_iota(jnp.int32, (LANES, LANES), 1)

    def to_row(col):
        return jnp.sum(jnp.where(eye, col, 0.0), axis=0, keepdims=True)

    def to_col(row):
        return jnp.sum(jnp.where(eye, row, 0.0), axis=1, keepdims=True)

    def tile(t):
        return pl.ds(pl.multiple_of(t * LANES, LANES), LANES)

    ssq[...] = jnp.zeros_like(ssq)
    for ref in (msg1, msg2, er, rr):
        ref[...] = jnp.zeros_like(ref)
    msg1[pl.ds(3 * rp, rt), :] = live_ref[...]

    locals_[0].wait()
    locals_[1].wait()
    ow = ow_ref[...]

    def student(t, carry):
        xt_ = xs[tile(t), :]
        cross = jnp.dot(xt_, cw[...], preferred_element_type=jnp.float32) + cb_ref[...]
        xf = xt_.astype(jnp.float32)
        m = xf * cross + xf
        mixed[tile(t), :] = m
        msg1[pl.ds(2 * rp + t, 1), :] = to_row(jnp.sum(m * ow, axis=1, keepdims=True))
        return carry

    lax.fori_loop(0, rt, student, 0)
    locals_[2].wait()
    locals_[3].wait()

    mt = row_count

    def project(dx, dy, dz):
        s = slot(dx, dy, dz)
        y_ = g if dy == 0 else 1 - g
        x_ = x if dx == 0 else 1 - x
        index = y_ * fsdp_count + (lax.rem(z + dz, nz) * 2 + x_) * 2 + core
        gains[pl.ds(s, 1), :] = gain_ref[index] * 0.5
        heads[pl.ds(s, 1), :] = head_ref[index]
        bias = bias_ref[index]

        def step(t, carry):
            ds = pl.ds(pl.multiple_of(t * mt, mt), mt)
            p = jnp.dot(rows[ds, :], wbuf[s], preferred_element_type=jnp.float32) + bias
            pre[s, ds, :] = p
            ssq[ds, :] += p * p
            return carry

        lax.fori_loop(0, 2 * row_count // mt, step, 0)

    lead = order[0]
    for h in range(2):
        diagonal(0, h)
        relay(lead, h)
    rows_in.wait_recv()
    project(0, 0, 0)
    along(lead, 0)
    project(1, 0, 0)
    project(0, 1, 0)

    xs_in.wait_recv()
    pick = (
        lax.broadcasted_iota(jnp.int32, (block, 2 * block), 1)
        == lax.broadcasted_iota(jnp.int32, (block, 2 * block), 0) + core * block
    )
    pick = jnp.where(pick, 1.0, 0.0).astype(jnp.bfloat16)
    for j in range(fsdp_count // 2):
        xt[pl.ds(j * block, block), :] = lax.dot_general(
            pick, xs[:, pl.ds(j * 2 * block, 2 * block)], (((1,), (1,)), ((), ())), preferred_element_type=jnp.float32
        ).astype(jnp.bfloat16)

    along(lead, 1)
    ready = [(1, 1, 0), (0, 0, lead)]
    late = []
    before = None
    for k in order[1:]:
        if before is not None:
            diagonal(before, 0)
        relay(k, 0)
        if before is not None:
            diagonal(before, 1)
            ready += [(1, 0, before), (0, 1, before)]
        else:
            for h in range(2):
                xin[lead, h].wait_recv()
                yin[lead, h].wait_recv()
            late += [(1, 0, lead), (0, 1, lead)]
        for item in ready:
            project(*item)
        relay(k, 1)
        ready = late + [(0, 0, k)]
        late = []
        before = k
    diagonal(before, 0)
    for item in ready:
        project(*item)
    for k in order[1:-1]:
        for h in range(2):
            arrived(k, h)
        project(1, 1, k)
    diagonal(before, 1)
    project(1, 0, before)
    project(0, 1, before)
    for k in (lead, before):
        for h in range(2):
            arrived(k, h)
        project(1, 1, k)

    for h in range(2):
        def squares(t, carry, h=h):
            col = jnp.sum(ssq[tile(h * rt + t), :], axis=1, keepdims=True)
            msg1[pl.ds(h * rp + t, 1), :] = to_row(col)
            return carry

        lax.fori_loop(0, rt, squares, 0)
    m1 = send(msg1, in1, partner)
    m1.wait_recv()
    for h in range(2):
        total = msg1[pl.ds(h * rp, rp), :] + in1[pl.ds((1 - h) * rp, rp), :]
        rr[pl.ds(h * rp, rp), :] = lax.rsqrt(total * (1.0 / units) + epsilon)

    for h in range(2):
        def logits(t, carry, h=h):
            r = to_col(rr[pl.ds(h * rp + t, 1), :])
            acc = jnp.zeros((LANES, LANES), jnp.float32)
            for s in range(4 * nz):
                v = pre[s, tile(h * rt + t), :] * r * gains[pl.ds(s, 1), :]
                acc += (v * jnp.tanh(v) + v) * heads[pl.ds(s, 1), :]
            msg2[pl.ds(h * rp + t, 1), :] = to_row(jnp.sum(acc, axis=1, keepdims=True))
            return carry

        lax.fori_loop(0, rt, logits, 0)
    m2 = send(msg2, in2, partner)
    m2.wait_recv()
    for h, src in ((0, msg1), (1, in1)):
        teacher = msg2[pl.ds(h * rp, rp), :] + in2[pl.ds((1 - h) * rp, rp), :]
        er[pl.ds(h * rp, rp), :] = (src[pl.ds(2 * rp, rp), :] - teacher) * src[pl.ds(3 * rp, rp), :]

    sb[...] = jnp.zeros_like(sb)

    def own(t, carry):
        e = to_col(er[pl.ds(t, 1), :])
        d = e * ow * xs[tile(t), :].astype(jnp.float32)
        dbuf[tile(t), :] = d.astype(jnp.bfloat16)
        sb[0, pl.ds(0, 1), :] += jnp.sum(d, axis=0, keepdims=True)
        sb[0, pl.ds(1, 1), :] += jnp.sum(e * mixed[tile(t), :], axis=0, keepdims=True)
        return carry

    lax.fori_loop(0, rt, own, 0)
    c0 = send(sb.at[0], rb.at[0], partner)

    def other(t, carry):
        e = to_col(er[pl.ds(rp + t, 1), :])
        d = e * ow * xs[tile(rt + t), :].astype(jnp.float32)
        dbuf[tile(rt + t), :] = d.astype(jnp.bfloat16)
        return carry

    lax.fori_loop(0, rt, other, 0)

    def way(p):
        return (g, x, yn, xn) if p % 2 == 0 else (x, g, xn, yn)

    h1, h2, h3, h4 = {}, {}, {}, {}

    def stage1(p):
        val = jnp.dot(xt[...], dbuf[:, pl.ds(p * pw, pw)], preferred_element_type=jnp.float32)
        for z_ in range(nz):
            for x_ in range(2):
                for y_ in range(2):
                    first, second = (y_, x_) if p % 2 == 0 else (x_, y_)
                    offset = ((z_ * 2 + x_) * 2 + y_) * half_rows
                    tw[p, first, second, z_] = val[offset:offset + half_rows, :]
        first, second, n1, n2 = way(p)
        h1[p] = send(tw.at[p, 1 - first], r1.at[p], n1)

    def stage2(p):
        first, second, n1, n2 = way(p)
        h1[p].wait_recv()
        s1[p] = tw[p, first] + r1[p]
        h2[p] = send(s1.at[p, 1 - second], r2.at[p], n2)

    def stage3(p):
        first, second, n1, n2 = way(p)
        h2[p].wait_recv()
        tt[p] = s1[p, second] + r2[p]
        h3[p] = []
        for k in range(1, nz):
            to = lax.rem(z + k, nz)
            h3[p].append(send(tt.at[p, to], r3.at[p, k - 1], at(g, to, x, core)))

    def stage4(p):
        total = tt[p, z]
        for k in range(nz - 1):
            h3[p][k].wait_recv()
            total = total + r3[p, k]
        fin[p] = total
        h4[p] = send(fin.at[p], r4.at[p], yn)
        out_ref[pl.ds(pl.multiple_of(g * half_rows, half_rows), half_rows), pl.ds(p * pw, pw)] = total

    cz = []

    def small(n):
        if n == 0:
            c0.wait_recv()
            sb[1] = sb[0] + rb[0]
            cz.append(send(sb.at[1], rb.at[1], xn))
        elif n == 1:
            cz.pop().wait_recv()
            sb[2] = sb[1] + rb[1]
            cz.append(send(sb.at[2], rb.at[2], yn))
        elif n == 2:
            cz.pop().wait_recv()
            sb[3] = sb[2] + rb[2]
            rz[z] = sb[3]
            for k in range(1, nz):
                to = lax.rem(z + k, nz)
                cz.append(send(sb.at[3], rz.at[z], at(g, to, x, core)))

    stages = (stage1, stage2, stage3, stage4)
    lag = (0, 2, 3, 5)
    for step in range(PAIRS + lag[-1]):
        for stage, behind in zip(stages, lag):
            q = step - behind
            if 0 <= q < PAIRS:
                stage(2 * q)
                stage(2 * q + 1)
        small(step - 1)
    for cp in cz:
        cp.wait_recv()
    total = rz[0]
    for k in range(1, nz):
        total = total + rz[k]
    small_ref[...] = total
    for p in range(parts):
        h4[p].wait_recv()
        out_ref[pl.ds(pl.multiple_of((1 - g) * half_rows, half_rows), half_rows), pl.ds(p * pw, pw)] = r4[p]
    for cp in sends:
        cp.wait_send()


def shards_fused(
    teacher_rows,
    student_rows,
    counts,
    teacher_weight,
    teacher_bias,
    teacher_gain,
    teacher_head,
    cross_weight,
    cross_bias,
    out_weight,
):
    row_count, fin_width = teacher_rows.shape
    width_s = cross_weight.shape[0]
    group_count = lax.axis_size("group")
    fsdp_count = lax.axis_size("fsdp")
    loss_scale = math.sqrt(width_s / (row_count * group_count * fsdp_count))
    live = (jnp.arange(row_count, dtype=jnp.int32) < counts[0]).astype(jnp.float32) * loss_scale
    rt = row_count // LANES
    rp = -(-rt // 8) * 8
    nz = fsdp_count // 4
    block = width_s // fsdp_count
    half_rows = block // 2
    parts = 2 * PAIRS
    pw = width_s // parts
    slots = 4 * nz
    f32, bf16 = jnp.float32, jnp.bfloat16
    vm = pltpu.VMEM
    split = lambda v: v.reshape(-1, 1, LANES)
    anyspec = pl.BlockSpec(memory_space=pl.ANY)
    vspec = pl.BlockSpec(memory_space=pltpu.VMEM)
    grad, small = pl.pallas_call(
        functools.partial(fused, fsdp_count, rp),
        out_shape=(jax.ShapeDtypeStruct((block, width_s), f32), jax.ShapeDtypeStruct((8, width_s), f32)),
        in_specs=[anyspec, anyspec, vspec, anyspec, vspec, vspec, vspec, anyspec, vspec, vspec],
        out_specs=(vspec, vspec),
        scratch_shapes=[
            vm((slots, fin_width, LANES), bf16),
            vm((2 * row_count, fin_width), bf16),
            vm((2 * row_count, width_s), bf16),
            vm((width_s, width_s), bf16),
            vm((slots, 2 * row_count, LANES), f32),
            vm((2 * row_count, LANES), f32),
            vm((slots, LANES), f32),
            vm((slots, LANES), f32),
            vm((row_count, width_s), f32),
            vm((4 * rp, LANES), f32),
            vm((4 * rp, LANES), f32),
            vm((2 * rp, LANES), f32),
            vm((2 * rp, LANES), f32),
            vm((2 * rp, LANES), f32),
            vm((2 * rp, LANES), f32),
            vm((width_s // 2, 2 * row_count), bf16),
            vm((2 * row_count, width_s), bf16),
            vm((parts, 2, 2, nz, half_rows, pw), f32),
            vm((parts, 2, nz, half_rows, pw), f32),
            vm((parts, 2, nz, half_rows, pw), f32),
            vm((parts, nz, half_rows, pw), f32),
            vm((parts, nz, half_rows, pw), f32),
            vm((parts, nz - 1, half_rows, pw), f32),
            vm((parts, half_rows, pw), f32),
            vm((parts, half_rows, pw), f32),
            vm((4, 8, width_s), f32),
            vm((3, 8, width_s), f32),
            vm((nz, 8, width_s), f32),
            pltpu.SemaphoreType.DMA((4,)),
            pltpu.SemaphoreType.DMA((SEMS,)),
            pltpu.SemaphoreType.DMA((SEMS,)),
        ],
        compiler_params=pltpu.CompilerParams(
            collective_id=0, has_side_effects=True, vmem_limit_bytes=60 * 1024 * 1024
        ),
    )(
        teacher_rows, student_rows, live.reshape(rt, LANES), teacher_weight, split(teacher_bias), split(teacher_gain),
        split(teacher_head), cross_weight, cross_bias[None, :], out_weight[None, :],
    )
    return (grad, small[0], small[1])


SEMS = 112


def fits(mesh, args):
    rows, fin_width = args[0].shape
    width_s = args[1].shape[1]
    units = args[3].shape[1]
    group_count, fsdp_count = mesh.shape["group"], mesh.shape["fsdp"]
    devices = group_count * fsdp_count
    return (
        group_count == 2
        and fsdp_count % 4 == 0
        and fsdp_count >= 8
        and fsdp_count <= 16
        and units == devices * LANES
        and (rows // devices) % LANES == 0
        and (2 * width_s // fsdp_count) % LANES == 0
        and width_s % (2 * PAIRS * LANES) == 0
    )


def solution(mesh):
    in_specs = (
        P(("group", "fsdp"), None),
        P(("group", "fsdp"), None),
        P(("group", "fsdp")),
        P(None, ("group", "fsdp")),
        P(),
        P(),
        P(),
        P(),
        P(),
        P(),
    )
    out_specs = (P("fsdp", None), P(), P())

    def run(*args):
        body = shards_fused if fits(mesh, args) else shards
        return jax.shard_map(body, mesh=mesh, in_specs=in_specs, out_specs=out_specs, check_vma=False)(*args)

    return run
```

profile of v0, /device:TPU:0, one launch (start us, length us, event | category | flops | bytes accessed | tf_op | source)
XLA Modules:
  0.0 129.2 jit_solution(3174893969620178440)
XLA Ops:
  1.3 0.6 fusion.live_ref
  1.9 124.2 %shard_map.121 = (f32[64,1024]{1,0:T(8,128)}, f32[8,1024]{1,0:T(8,128)}) custom-call(bf16[640,2048]{1,0:T(8,128)(2,1)} %t_ref.1, bf16[640,1024]{1,0:T(8,128)(2,1)} %s_ref.1, f32[5,128]{1,0:T(8,128)} %fusion.live_ref, bf16[2048,128]{1,0:T(8,128)(2,1)} %w_ref.1, f32[32,1,128]{2,1,0:T(1,128)} %bitcast.9, f32[32,1,128]{2,1,0:T(1,128)} %bitcast.10, ...), custom_call_target="tpu_custom_call" | custom-call | tf_op jit(solution)/shard_map/pallas_call | solution.py:439
  126.1 1.4 %fusion.1 = (f32[1,1024]{1,0:T(1,128)}, f32[1,1024]{1,0:T(1,128)}) fusion(f32[8,1024]{1,0:T(8,128)} %get-tuple-element.6), kind=kLoop, calls=%fused_computation.2 | loop fusion | bytes 16384 | tf_op jit(solution)/shard_map/slice | solution.py:484
  127.6 1.7 %copy.15 = f32[64,1024]{1,0:T(8,128)} copy(f32[64,1024]{1,0:T(8,128)} %get-tuple-element.12) | data formatting | bytes 524288
where the time goes:
time: 130 us; the launch traced here: 129 us
  Pallas kernels  124 us (95%)
  local copies, waits for them, and re-layouts  3.11 us (2%)
    pallas_call x1, Pallas kernels, shards_fused(): pl.pallas_call(functools.partial(fused, fsdp_count, rp), out_shape=(jax.S...  124 us

commit v1 on v0

--- a/solution.py
+++ b/solution.py
@@ -60,12 +60,13 @@
 MESH = pl.DeviceIdType.MESH
 LANES = 128
 PAIRS = 4
+QUARTERS = 4
 
 
 def fused(fsdp_count, rp, t_ref, s_ref, live_ref, w_ref, bias_ref, gain_ref, head_ref, cw_ref, cb_ref, ow_ref,
           out_ref, small_ref,
           wbuf, rows, xs, cw, pre, ssq, gains, heads, mixed, msg1, in1, msg2, in2, rr, er, xt, dbuf,
-          tw, r1, s1, r2, tt, r3, fin, r4, sb, rb, rz, lsem, ssem, rsem):
+          tw, r1, s1, r2, tt, r3, fin, r4, sb, rb, rz, lsem, ssem, rsem, wsem):
     g = lax.axis_index("group")
     f = lax.axis_index("fsdp")
     core = lax.rem(f, 2)
@@ -105,62 +106,84 @@
     pl.semaphore_wait(barrier, len(peers))
 
     sends = []
-
-    def send(a, b, device):
-        i = len(sends)
+    mid_sends = []
+    waits = []
+    turn = [0]
+
+    def send(a, b, device, recv=None, only_mid=False):
+        i = turn[0]
+        turn[0] += 1
+        if recv is None:
+            recv = rsem.at[len(waits)]
+            waits.append(i)
         cp = pltpu.make_async_remote_copy(
-            src_ref=a, dst_ref=b, send_sem=ssem.at[i], recv_sem=rsem.at[i], device_id=device, device_id_type=MESH
+            src_ref=a, dst_ref=b, send_sem=ssem.at[i], recv_sem=recv, device_id=device, device_id_type=MESH
         )
         cp.start()
-        sends.append(cp)
+        if only_mid:
+            mid_sends.append(i)
+        else:
+            sends.append(cp)
         return cp
 
-    def slot(dx, dy, dz):
-        return (dx * 2 + dy) * nz + dz
-
-    order = [1] + list(range(nz - 1, 1, -1))
-    depth = fin_width // 2
-    xin, yin, zin, din = {}, {}, {}, {}
-
-    def half(ref, h):
-        return ref.at[pl.ds(h * depth, depth)]
-
-    def piece(dx, dy, dz, h):
-        return wbuf.at[slot(dx, dy, dz), pl.ds(h * depth, depth)]
-
-    def zpeer(k):
-        return at(g, lax.rem(z + nz - k, nz), x, core)
-
-    for h in range(2):
-        xin[0, h] = send(half(w_ref, h), piece(1, 0, 0, h), xn)
-        yin[0, h] = send(half(w_ref, h), piece(0, 1, 0, h), yn)
-        zin[order[0], h] = send(half(w_ref, h), piece(0, 0, order[0], h), zpeer(order[0]))
-    for k in order[1:]:
-        for h in range(2):
-            zin[k, h] = send(half(w_ref, h), piece(0, 0, k, h), zpeer(k))
+    half_z = lax.div(z, 2)
+    is_mid = jnp.logical_or(z == 1, z == 2)
+    is_end = jnp.logical_not(is_mid)
+    plane = (z, z + 1 - 2 * lax.rem(z, 2), 2 - half_z, 3 - 3 * half_z)
+    zpair = at(g, plane[1], x, core)
+    zmid = at(g, nz - 1 - z, x, core)
+    depth = fin_width // QUARTERS
+    quarters = list(range(QUARTERS))
+    first, last = quarters[:QUARTERS // 2], quarters[QUARTERS // 2:]
+
+    def slot(dx, dy, n):
+        return (dx * 2 + dy) * nz + n
+
+    def piece(dx, dy, n, q):
+        return wbuf.at[slot(dx, dy, n), pl.ds(q * depth, depth)]
+
+    def arrival(dx, dy, n, q):
+        return wsem.at[slot(dx, dy, n) * QUARTERS + q]
+
+    def pass_on(src, dst, q, device, only_mid=False):
+        here = w_ref.at[pl.ds(q * depth, depth)] if src is None else piece(*src, q)
+        send(here, piece(*dst, q), device, arrival(*dst, q), only_mid)
+
+    def landed(dx, dy, n, qs):
+        for q in qs:
+            pltpu.make_async_remote_copy(
+                src_ref=piece(dx, dy, n, q), dst_ref=piece(dx, dy, n, q), send_sem=ssem.at[0],
+                recv_sem=arrival(dx, dy, n, q), device_id=partner, device_id_type=MESH
+            ).wait_recv()
+
+    def sideways(src, n):
+        for qx, qy in zip(last + first, quarters):
+            pass_on(src, (1, 0, n), qx, xn)
+            pass_on(src, (0, 1, n), qy, yn)
+
+    for qx, q in zip(last + first, quarters):
+        pass_on(None, (1, 0, 0), qx, xn)
+        pass_on(None, (0, 1, 0), q, yn)
+        pass_on(None, (0, 0, 1), q, zpair)
+
+    @pl.when(is_mid)
+    def _():
+        for q in quarters:
+            pass_on(None, (0, 0, 2), q, zmid, True)
+
     rows_in = send(t_ref, rows.at[pl.ds(row_count, row_count)], partner)
     xs_in = send(s_ref, xs.at[pl.ds(row_count, row_count)], partner)
 
-    def diagonal(k, h):
-        lo, hi = pl.ds(h * depth, depth // 2), pl.ds(h * depth + depth // 2, depth // 2)
-        xin[k, h].wait_recv()
-        a = send(wbuf.at[slot(1, 0, k), lo], wbuf.at[slot(1, 1, k), lo], yn)
-        yin[k, h].wait_recv()
-        b = send(wbuf.at[slot(0, 1, k), hi], wbuf.at[slot(1, 1, k), hi], xn)
-        din[k, h] = (a, b)
-
-    def relay(k, h):
-        zin[k, h].wait_recv()
-        xin[k, h] = send(piece(0, 0, k, h), piece(1, 0, k, h), xn)
-        yin[k, h] = send(piece(0, 0, k, h), piece(0, 1, k, h), yn)
-
-    def arrived(k, h):
-        for cp in din[k, h]:
-            cp.wait_recv()
-
-    def along(k, h):
-        arrived(0, h)
-        din[k, h] = (send(piece(1, 1, 0, h), piece(1, 1, k, h), zpeer(k)),)
+    def diagonal(n):
+        for qx, qy in zip(first, last):
+            landed(0, 1, n, [qx])
+            pass_on((0, 1, n), (1, 1, n), qx, xn)
+            landed(1, 0, n, [qy])
+            pass_on((1, 0, n), (1, 1, n), qy, yn)
+
+    def rest(n):
+        landed(0, 1, n, last)
+        landed(1, 0, n, first)
 
     eye = lax.broadcasted_iota(jnp.int32, (LANES, LANES), 0) == lax.broadcasted_iota(jnp.int32, (LANES, LANES), 1)
 
@@ -197,11 +220,11 @@
 
     mt = row_count
 
-    def project(dx, dy, dz):
-        s = slot(dx, dy, dz)
+    def project(dx, dy, n):
+        s = slot(dx, dy, n)
         y_ = g if dy == 0 else 1 - g
         x_ = x if dx == 0 else 1 - x
-        index = y_ * fsdp_count + (lax.rem(z + dz, nz) * 2 + x_) * 2 + core
+        index = y_ * fsdp_count + (plane[n] * 2 + x_) * 2 + core
         gains[pl.ds(s, 1), :] = gain_ref[index] * 0.5
         heads[pl.ds(s, 1), :] = head_ref[index]
         bias = bias_ref[index]
@@ -215,15 +238,35 @@
 
         lax.fori_loop(0, 2 * row_count // mt, step, 0)
 
-    lead = order[0]
-    for h in range(2):
-        diagonal(0, h)
-        relay(lead, h)
     rows_in.wait_recv()
     project(0, 0, 0)
-    along(lead, 0)
+    diagonal(0)
+
+    @pl.when(is_mid)
+    def _():
+        for q in quarters:
+            landed(0, 0, 2, [q])
+            pass_on((0, 0, 2), (0, 0, 2), q, zpair, True)
+
+    for q in quarters:
+        landed(0, 0, 1, [q])
+
+        @pl.when(is_mid)
+        def _(q=q):
+            pass_on((0, 0, 1), (0, 0, 3), q, zmid, True)
+
+    sideways((0, 0, 1), 1)
+    rest(0)
     project(1, 0, 0)
     project(0, 1, 0)
+    project(0, 0, 1)
+    for q in [q for pair in zip(first, last) for q in pair]:
+        landed(1, 1, 0, [q])
+        pass_on((1, 1, 0), (1, 1, 1), q, zpair)
+
+        @pl.when(is_mid)
+        def _(q=q):
+            pass_on((1, 1, 0), (1, 1, 2), q, zmid, True)
 
     xs_in.wait_recv()
     pick = (
@@ -236,42 +279,54 @@
             pick, xs[:, pl.ds(j * 2 * block, 2 * block)], (((1,), (1,)), ((), ())), preferred_element_type=jnp.float32
         ).astype(jnp.bfloat16)
 
-    along(lead, 1)
-    ready = [(1, 1, 0), (0, 0, lead)]
-    late = []
-    before = None
-    for k in order[1:]:
-        if before is not None:
-            diagonal(before, 0)
-        relay(k, 0)
-        if before is not None:
-            diagonal(before, 1)
-            ready += [(1, 0, before), (0, 1, before)]
-        else:
-            for h in range(2):
-                xin[lead, h].wait_recv()
-                yin[lead, h].wait_recv()
-            late += [(1, 0, lead), (0, 1, lead)]
-        for item in ready:
-            project(*item)
-        relay(k, 1)
-        ready = late + [(0, 0, k)]
-        late = []
-        before = k
-    diagonal(before, 0)
-    for item in ready:
-        project(*item)
-    for k in order[1:-1]:
-        for h in range(2):
-            arrived(k, h)
-        project(1, 1, k)
-    diagonal(before, 1)
-    project(1, 0, before)
-    project(0, 1, before)
-    for k in (lead, before):
-        for h in range(2):
-            arrived(k, h)
-        project(1, 1, k)
+    @pl.when(is_mid)
+    def _():
+        for q in quarters:
+            landed(0, 0, 3, [q])
+            pass_on((0, 0, 3), (0, 0, 3), q, zpair, True)
+
+    project(1, 1, 0)
+
+    @pl.when(is_end)
+    def _():
+        landed(0, 0, 2, quarters)
+
+    sideways((0, 0, 2), 2)
+    project(0, 0, 2)
+    for at_ in ((1, 0, 1), (0, 1, 1)):
+        landed(*at_, quarters)
+        project(*at_)
+
+    @pl.when(is_end)
+    def _():
+        landed(0, 0, 3, quarters)
+
+    sideways((0, 0, 3), 3)
+
+    @pl.when(is_mid)
+    def _():
+        for q in quarters:
+            landed(1, 1, 2, [q])
+            pass_on((1, 1, 2), (1, 1, 2), q, zpair, True)
+
+    project(0, 0, 3)
+    for at_ in ((1, 0, 2), (0, 1, 2)):
+        landed(*at_, quarters)
+        project(*at_)
+    diagonal(3)
+    landed(1, 1, 1, quarters)
+    project(1, 1, 1)
+    rest(3)
+    project(1, 0, 3)
+    project(0, 1, 3)
+
+    @pl.when(is_end)
+    def _():
+        landed(1, 1, 2, quarters)
+
+    project(1, 1, 2)
+    landed(1, 1, 3, quarters)
+    project(1, 1, 3)
 
     for h in range(2):
         def squares(t, carry, h=h):
@@ -403,6 +458,14 @@
         out_ref[pl.ds(pl.multiple_of((1 - g) * half_rows, half_rows), half_rows), pl.ds(p * pw, pw)] = r4[p]
     for cp in sends:
         cp.wait_send()
+
+    @pl.when(is_mid)
+    def _():
+        for i in mid_sends:
+            pltpu.make_async_remote_copy(
+                src_ref=piece(0, 0, 0, 0), dst_ref=piece(0, 0, 0, 0), send_sem=ssem.at[i], recv_sem=wsem.at[0],
+                device_id=partner, device_id_type=MESH
+            ).wait_send()
 
 
 def shards_fused(
@@ -471,8 +534,9 @@
             vm((3, 8, width_s), f32),
             vm((nz, 8, width_s), f32),
             pltpu.SemaphoreType.DMA((4,)),
-            pltpu.SemaphoreType.DMA((SEMS,)),
-            pltpu.SemaphoreType.DMA((SEMS,)),
+            pltpu.SemaphoreType.DMA((SENDS,)),
+            pltpu.SemaphoreType.DMA((OTHERS,)),
+            pltpu.SemaphoreType.DMA((slots * QUARTERS,)),
         ],
         compiler_params=pltpu.CompilerParams(
             collective_id=0, has_side_effects=True, vmem_limit_bytes=60 * 1024 * 1024
@@ -484,7 +548,8 @@
     return (grad, small[0], small[1])
 
 
-SEMS = 112
+SENDS = 160
+OTHERS = 72
 
 
 def fits(mesh, args):
@@ -495,9 +560,7 @@
     devices = group_count * fsdp_count
     return (
         group_count == 2
-        and fsdp_count % 4 == 0
-        and fsdp_count >= 8
-        and fsdp_count <= 16
+        and fsdp_count == 16
         and units == devices * LANES
         and (rows // devices) % LANES == 0
         and (2 * width_s // fsdp_count) % LANES == 0

time: 130 us -> 121 us (0.931)
  Pallas kernels: 124 us -> 116 us
    pallas_call x1, Pallas kernels: 124 us -> 116 us  [shards_fused(): pl.pallas_call(functools.partial(fused, fsdp_count, rp), out_shape=(jax.S...]
where the time goes in v1:
time: 121 us; the launch traced here: 120 us
  Pallas kernels  116 us (96%)
  local copies, waits for them, and re-layouts  3.11 us (3%)
  between operations  1.29 us (1%)
    pallas_call x1, Pallas kernels, shards_fused(): pl.pallas_call(functools.partial(fused, fsdp_count, rp), out_shape=(jax.S...  116 us

profile of v1, /device:TPU:0, one launch (start us, length us, event | category | flops | bytes accessed | tf_op | source)
XLA Modules:
  0.0 120.5 jit_solution(16114677535766368189)
XLA Ops:
  1.3 0.6 fusion.live_ref
  1.9 115.5 %shard_map.121 = (f32[64,1024]{1,0:T(8,128)}, f32[8,1024]{1,0:T(8,128)}) custom-call(bf16[640,2048]{1,0:T(8,128)(2,1)} %t_ref.1, bf16[640,1024]{1,0:T(8,128)(2,1)} %s_ref.1, f32[5,128]{1,0:T(8,128)} %fusion.live_ref, bf16[2048,128]{1,0:T(8,128)(2,1)} %w_ref.1, f32[32,1,128]{2,1,0:T(1,128)} %bitcast.9, f32[32,1,128]{2,1,0:T(1,128)} %bitcast.10, ...), custom_call_target="tpu_custom_call" | custom-call | tf_op jit(solution)/shard_map/pallas_call | solution.py:502
  117.4 1.4 %fusion.1 = (f32[1,1024]{1,0:T(1,128)}, f32[1,1024]{1,0:T(1,128)}) fusion(f32[8,1024]{1,0:T(8,128)} %get-tuple-element.6), kind=kLoop, calls=%fused_computation.2 | loop fusion | bytes 16384 | tf_op jit(solution)/shard_map/slice | solution.py:548
  118.8 1.7 %copy.15 = f32[64,1024]{1,0:T(8,128)} copy(f32[64,1024]{1,0:T(8,128)} %get-tuple-element.12) | data formatting | bytes 524288

commit v2 on v1

--- a/solution.py
+++ b/solution.py
@@ -107,10 +107,11 @@
 
     sends = []
     mid_sends = []
+    end_sends = []
     waits = []
     turn = [0]
 
-    def send(a, b, device, recv=None, only_mid=False):
+    def send(a, b, device, recv=None, only=None):
         i = turn[0]
         turn[0] += 1
         if recv is None:
@@ -120,8 +121,8 @@
             src_ref=a, dst_ref=b, send_sem=ssem.at[i], recv_sem=recv, device_id=device, device_id_type=MESH
         )
         cp.start()
-        if only_mid:
-            mid_sends.append(i)
+        if only:
+            (end_sends if only == 'end' else mid_sends).append(i)
         else:
             sends.append(cp)
         return cp
@@ -145,9 +146,9 @@
     def arrival(dx, dy, n, q):
         return wsem.at[slot(dx, dy, n) * QUARTERS + q]
 
-    def pass_on(src, dst, q, device, only_mid=False):
+    def pass_on(src, dst, q, device, only=None):
         here = w_ref.at[pl.ds(q * depth, depth)] if src is None else piece(*src, q)
-        send(here, piece(*dst, q), device, arrival(*dst, q), only_mid)
+        send(here, piece(*dst, q), device, arrival(*dst, q), only)
 
     def landed(dx, dy, n, qs):
         for q in qs:
@@ -169,7 +170,7 @@
     @pl.when(is_mid)
     def _():
         for q in quarters:
-            pass_on(None, (0, 0, 2), q, zmid, True)
+            pass_on(None, (0, 0, 2), q, zmid, 'mid')
 
     rows_in = send(t_ref, rows.at[pl.ds(row_count, row_count)], partner)
     xs_in = send(s_ref, xs.at[pl.ds(row_count, row_count)], partner)
@@ -238,36 +239,56 @@
 
         lax.fori_loop(0, 2 * row_count // mt, step, 0)
 
+    order = [q for pair in zip(first, last) for q in pair]
+
+    for i, (qx, qy) in enumerate(zip(first, last)):
+        landed(0, 1, 0, [qx])
+        pass_on((0, 1, 0), (1, 1, 0), qx, xn)
+        landed(1, 0, 0, [qy])
+        pass_on((1, 0, 0), (1, 1, 0), qy, yn)
+
+        @pl.when(is_mid)
+        def _(i=i):
+            for q in quarters[2 * i:2 * i + 2]:
+                landed(0, 0, 2, [q])
+                pass_on((0, 0, 2), (0, 0, 2), q, zpair, 'mid')
+                landed(0, 0, 1, [q])
+                pass_on((0, 0, 1), (0, 0, 3), q, zmid, 'mid')
+
     rows_in.wait_recv()
     project(0, 0, 0)
-    diagonal(0)
-
-    @pl.when(is_mid)
-    def _():
-        for q in quarters:
-            landed(0, 0, 2, [q])
-            pass_on((0, 0, 2), (0, 0, 2), q, zpair, True)
-
-    for q in quarters:
-        landed(0, 0, 1, [q])
-
-        @pl.when(is_mid)
-        def _(q=q):
-            pass_on((0, 0, 1), (0, 0, 3), q, zmid, True)
+
+    @pl.when(is_end)
+    def _():
+        landed(0, 0, 1, quarters)
 
     sideways((0, 0, 1), 1)
     rest(0)
     project(1, 0, 0)
+
+    def far(q):
+        landed(0, 0, 3, [q])
+        pass_on((0, 0, 3), (0, 0, 3), q, zpair, 'mid')
+
+    @pl.when(is_mid)
+    def _():
+        far(0)
+
     project(0, 1, 0)
+    for i, q in enumerate(order):
+        landed(1, 1, 0, [q])
+
+        @pl.when(is_end)
+        def _(q=q):
+            pass_on((1, 1, 0), (1, 1, 1), q, zpair, 'end')
+
+        @pl.when(is_mid)
+        def _(q=q, i=i):
+            pass_on((1, 1, 0), (1, 1, 2), q, zmid, 'mid')
+            if i == 1:
+                far(1)
+
     project(0, 0, 1)
-    for q in [q for pair in zip(first, last) for q in pair]:
-        landed(1, 1, 0, [q])
-        pass_on((1, 1, 0), (1, 1, 1), q, zpair)
-
-        @pl.when(is_mid)
-        def _(q=q):
-            pass_on((1, 1, 0), (1, 1, 2), q, zmid, True)
-
     xs_in.wait_recv()
     pick = (
         lax.broadcasted_iota(jnp.int32, (block, 2 * block), 1)
@@ -281,33 +302,34 @@
 
     @pl.when(is_mid)
     def _():
-        for q in quarters:
-            landed(0, 0, 3, [q])
-            pass_on((0, 0, 3), (0, 0, 3), q, zpair, True)
-
+        for q in quarters[2:]:
+            far(q)
+        for q in order:
+            pass_on((1, 1, 0), (1, 1, 1), q, zpair, 'mid')
+
+    @pl.when(is_end)
+    def _():
+        landed(0, 0, 2, quarters)
+
+    sideways((0, 0, 2), 2)
     project(1, 1, 0)
+    project(0, 0, 2)
+    landed(1, 0, 1, quarters)
+    project(1, 0, 1)
+    landed(0, 1, 1, quarters)
 
     @pl.when(is_end)
     def _():
-        landed(0, 0, 2, quarters)
-
-    sideways((0, 0, 2), 2)
-    project(0, 0, 2)
-    for at_ in ((1, 0, 1), (0, 1, 1)):
-        landed(*at_, quarters)
-        project(*at_)
-
-    @pl.when(is_end)
-    def _():
         landed(0, 0, 3, quarters)
 
     sideways((0, 0, 3), 3)
+    project(0, 1, 1)
 
     @pl.when(is_mid)
     def _():
-        for q in quarters:
+        for q in order:
             landed(1, 1, 2, [q])
-            pass_on((1, 1, 2), (1, 1, 2), q, zpair, True)
+            pass_on((1, 1, 2), (1, 1, 2), q, zpair, 'mid')
 
     project(0, 0, 3)
     for at_ in ((1, 0, 2), (0, 1, 2)):
@@ -459,13 +481,14 @@
     for cp in sends:
         cp.wait_send()
 
-    @pl.when(is_mid)
-    def _():
-        for i in mid_sends:
-            pltpu.make_async_remote_copy(
-                src_ref=piece(0, 0, 0, 0), dst_ref=piece(0, 0, 0, 0), send_sem=ssem.at[i], recv_sem=wsem.at[0],
-                device_id=partner, device_id_type=MESH
-            ).wait_send()
+    for kind, some in ((is_mid, mid_sends), (is_end, end_sends)):
+        @pl.when(kind)
+        def _(some=some):
+            for i in some:
+                pltpu.make_async_remote_copy(
+                    src_ref=piece(0, 0, 0, 0), dst_ref=piece(0, 0, 0, 0), send_sem=ssem.at[i], recv_sem=wsem.at[0],
+                    device_id=partner, device_id_type=MESH
+                ).wait_send()
 
 
 def shards_fused(

time: 121 us -> 115 us (0.950)
  Pallas kernels: 116 us -> 110 us
    pallas_call x1, Pallas kernels: 116 us -> 110 us  [shards_fused(): pl.pallas_call(functools.partial(fused, fsdp_count, rp), out_shape=(jax.S...]
where the time goes in v2:
time: 115 us
  Pallas kernels  110 us (96%)
  local copies, waits for them, and re-layouts  3.11 us (3%)
  between operations  1.29 us (1%)
    pallas_call x1, Pallas kernels, shards_fused(): pl.pallas_call(functools.partial(fused, fsdp_count, rp), out_shape=(jax.S...  110 us

profile of v2, /device:TPU:0, one launch (start us, length us, event | category | flops | bytes accessed | tf_op | source)
XLA Modules:
  0.0 115.0 jit_solution(10668026287462593321)
XLA Ops:
  1.3 0.6 fusion.live_ref
  1.9 110.0 %shard_map.121 = (f32[64,1024]{1,0:T(8,128)}, f32[8,1024]{1,0:T(8,128)}) custom-call(bf16[640,2048]{1,0:T(8,128)(2,1)} %t_ref.1, bf16[640,1024]{1,0:T(8,128)(2,1)} %s_ref.1, f32[5,128]{1,0:T(8,128)} %fusion.live_ref, bf16[2048,128]{1,0:T(8,128)(2,1)} %w_ref.1, f32[32,1,128]{2,1,0:T(1,128)} %bitcast.9, f32[32,1,128]{2,1,0:T(1,128)} %bitcast.10, ...), custom_call_target="tpu_custom_call" | custom-call | tf_op jit(solution)/shard_map/pallas_call | solution.py:525
  111.8 1.4 %fusion.1 = (f32[1,1024]{1,0:T(1,128)}, f32[1,1024]{1,0:T(1,128)}) fusion(f32[8,1024]{1,0:T(8,128)} %get-tuple-element.6), kind=kLoop, calls=%fused_computation.2 | loop fusion | bytes 16384 | tf_op jit(solution)/shard_map/slice | solution.py:571
  113.3 1.7 %copy.15 = f32[64,1024]{1,0:T(8,128)} copy(f32[64,1024]{1,0:T(8,128)} %get-tuple-element.12) | data formatting | bytes 524288

commit v3 on v2

--- a/solution.py
+++ b/solution.py
@@ -61,12 +61,19 @@
 LANES = 128
 PAIRS = 4
 QUARTERS = 4
+CODE_ROWS = 16
+CODE_BITS = 15.0
+CODE_MOST = 32767.0
+PLAN = (
+    (1, 0), (1, 1), (0, 0), (1, 2), (2, 0), (1, 3), (0, 1), (2, 1), (3, 0), (0, 2), (2, 2), (3, 1), (2, 3), (0, 3), (3, 2), (4, 0),
+    (3, 3), (4, 1), (4, 2), (4, 3),
+)
 
 
 def fused(fsdp_count, rp, t_ref, s_ref, live_ref, w_ref, bias_ref, gain_ref, head_ref, cw_ref, cb_ref, ow_ref,
           out_ref, small_ref,
           wbuf, rows, xs, cw, pre, ssq, gains, heads, mixed, msg1, in1, msg2, in2, rr, er, xt, dbuf,
-          tw, r1, s1, r2, tt, r3, fin, r4, sb, rb, rz, lsem, ssem, rsem, wsem):
+          ecol, tw, q1, r1, s1, q2, r2, tt, q3, r3, fin, r4, sb, rb, rz, lsem, ssem, rsem, wsem):
     g = lax.axis_index("group")
     f = lax.axis_index("fsdp")
     core = lax.rem(f, 2)
@@ -380,72 +387,115 @@
         teacher = msg2[pl.ds(h * rp, rp), :] + in2[pl.ds((1 - h) * rp, rp), :]
         er[pl.ds(h * rp, rp), :] = (src[pl.ds(2 * rp, rp), :] - teacher) * src[pl.ds(3 * rp, rp), :]
 
+    def spread(t, carry):
+        ecol[tile(t), :] = jnp.broadcast_to(to_col(er[pl.ds(t, 1), :]), (LANES, LANES))
+        ecol[tile(rt + t), :] = jnp.broadcast_to(to_col(er[pl.ds(rp + t, 1), :]), (LANES, LANES))
+        return carry
+
+    lax.fori_loop(0, rt, spread, 0)
     sb[...] = jnp.zeros_like(sb)
 
-    def own(t, carry):
-        e = to_col(er[pl.ds(t, 1), :])
-        d = e * ow * xs[tile(t), :].astype(jnp.float32)
-        dbuf[tile(t), :] = d.astype(jnp.bfloat16)
-        sb[0, pl.ds(0, 1), :] += jnp.sum(d, axis=0, keepdims=True)
-        sb[0, pl.ds(1, 1), :] += jnp.sum(e * mixed[tile(t), :], axis=0, keepdims=True)
-        return carry
-
-    lax.fori_loop(0, rt, own, 0)
-    c0 = send(sb.at[0], rb.at[0], partner)
-
-    def other(t, carry):
-        e = to_col(er[pl.ds(rp + t, 1), :])
-        d = e * ow * xs[tile(rt + t), :].astype(jnp.float32)
-        dbuf[tile(rt + t), :] = d.astype(jnp.bfloat16)
-        return carry
-
-    lax.fori_loop(0, rt, other, 0)
+    def scale_cross(p):
+        cols = pl.ds(p * pw, pw)
+        owp = ow_ref[:, cols]
+
+        def cross_tile(t, carry):
+            d = ecol[tile(t), :] * owp * xs[tile(t), cols].astype(jnp.float32)
+            dbuf[tile(t), cols] = d.astype(jnp.bfloat16)
+            return carry
+
+        lax.fori_loop(0, 2 * rt, cross_tile, 0)
+
+    def small_terms():
+        def one(t, carry):
+            for p in range(parts):
+                cols = pl.ds(p * pw, pw)
+                e = ecol[tile(t), :]
+                d = e * ow_ref[:, cols] * xs[tile(t), cols].astype(jnp.float32)
+                sb[0, pl.ds(0, 1), cols] += jnp.sum(d, axis=0, keepdims=True)
+                sb[0, pl.ds(1, 1), cols] += jnp.sum(e * mixed[tile(t), cols], axis=0, keepdims=True)
+            return carry
+
+        lax.fori_loop(0, rt, one, 0)
+
+    exp_row = lax.broadcasted_iota(jnp.int32, (CODE_ROWS, pw), 0)
+
+    def encode(blocks, msg):
+        exps = jnp.zeros((CODE_ROWS, pw), jnp.float32)
+        for i, v in enumerate(blocks):
+            most = jnp.max(jnp.abs(v), axis=0, keepdims=True)
+            e = jnp.ceil(jnp.log2(jnp.maximum(most, 1e-30)))
+            exps = jnp.where(exp_row == i, e, exps)
+            q = jnp.clip(jnp.round(v * jnp.exp2(CODE_BITS - e)), -CODE_MOST, CODE_MOST)
+            msg[pl.ds(i * half_rows, half_rows), :] = q.astype(jnp.int32).astype(jnp.int16)
+        msg[pl.ds(len(blocks) * half_rows, CODE_ROWS), :] = exps.astype(jnp.int32).astype(jnp.int16)
+
+    def decode(msg, n):
+        exps = msg[pl.ds(n * half_rows, CODE_ROWS), :].astype(jnp.int32).astype(jnp.float32)
+        step = jnp.exp2(exps - CODE_BITS)
+        out = []
+        for i in range(n):
+            q = msg[pl.ds(i * half_rows, half_rows), :].astype(jnp.int32).astype(jnp.float32)
+            out.append(q * step[i:i + 1, :])
+        return out
 
     def way(p):
         return (g, x, yn, xn) if p % 2 == 0 else (x, g, xn, yn)
 
     h1, h2, h3, h4 = {}, {}, {}, {}
 
-    def stage1(p):
-        val = jnp.dot(xt[...], dbuf[:, pl.ds(p * pw, pw)], preferred_element_type=jnp.float32)
+    def stage1(q):
+        for p in (2 * q, 2 * q + 1):
+            scale_cross(p)
+            val = jnp.dot(xt[...], dbuf[:, pl.ds(p * pw, pw)], preferred_element_type=jnp.float32)
+            for z_ in range(nz):
+                for x_ in range(2):
+                    for y_ in range(2):
+                        first, second = (y_, x_) if p % 2 == 0 else (x_, y_)
+                        offset = ((z_ * 2 + x_) * 2 + y_) * half_rows
+                        tw[p, first, second, z_] = val[offset:offset + half_rows, :]
+            first, second, n1, n2 = way(p)
+            encode([tw[p, 1 - first, s_, z_] for s_ in range(2) for z_ in range(nz)], q1.at[p])
+            h1[p] = send(q1.at[p], r1.at[p], n1)
+
+    def stage2(q):
+        for p in (2 * q, 2 * q + 1):
+            first, second, n1, n2 = way(p)
+            h1[p].wait_recv()
+            for i, v in enumerate(decode(r1.at[p], 2 * nz)):
+                s1[p, i // nz, i % nz] = tw[p, first, i // nz, i % nz] + v
+            encode([s1[p, 1 - second, z_] for z_ in range(nz)], q2.at[p])
+            h2[p] = send(q2.at[p], r2.at[p], n2)
+
+    def stage3(q):
+        for p in (2 * q, 2 * q + 1):
+            first, second, n1, n2 = way(p)
+            h2[p].wait_recv()
+            for z_, v in enumerate(decode(r2.at[p], nz)):
+                tt[p, z_] = s1[p, second, z_] + v
         for z_ in range(nz):
-            for x_ in range(2):
-                for y_ in range(2):
-                    first, second = (y_, x_) if p % 2 == 0 else (x_, y_)
-                    offset = ((z_ * 2 + x_) * 2 + y_) * half_rows
-                    tw[p, first, second, z_] = val[offset:offset + half_rows, :]
-        first, second, n1, n2 = way(p)
-        h1[p] = send(tw.at[p, 1 - first], r1.at[p], n1)
-
-    def stage2(p):
-        first, second, n1, n2 = way(p)
-        h1[p].wait_recv()
-        s1[p] = tw[p, first] + r1[p]
-        h2[p] = send(s1.at[p, 1 - second], r2.at[p], n2)
-
-    def stage3(p):
-        first, second, n1, n2 = way(p)
-        h2[p].wait_recv()
-        tt[p] = s1[p, second] + r2[p]
-        h3[p] = []
+            encode([tt[2 * q, z_], tt[2 * q + 1, z_]], q3.at[q, z_])
+        h3[q] = []
         for k in range(1, nz):
             to = lax.rem(z + k, nz)
-            h3[p].append(send(tt.at[p, to], r3.at[p, k - 1], at(g, to, x, core)))
-
-    def stage4(p):
-        total = tt[p, z]
+            h3[q].append(send(q3.at[q, to], r3.at[q, k - 1], at(g, to, x, core)))
+
+    def stage4(q):
+        totals = [tt[2 * q, z], tt[2 * q + 1, z]]
         for k in range(nz - 1):
-            h3[p][k].wait_recv()
-            total = total + r3[p, k]
-        fin[p] = total
-        h4[p] = send(fin.at[p], r4.at[p], yn)
-        out_ref[pl.ds(pl.multiple_of(g * half_rows, half_rows), half_rows), pl.ds(p * pw, pw)] = total
+            h3[q][k].wait_recv()
+            totals = [t + v for t, v in zip(totals, decode(r3.at[q, k], 2))]
+        for i, total in enumerate(totals):
+            p = 2 * q + i
+            fin[q, :, pl.ds(i * pw, pw)] = total
+            out_ref[pl.ds(pl.multiple_of(g * half_rows, half_rows), half_rows), pl.ds(p * pw, pw)] = total
+        h4[q] = send(fin.at[q], r4.at[q], yn)
 
     cz = []
 
     def small(n):
         if n == 0:
-            c0.wait_recv()
+            cz.pop().wait_recv()
             sb[1] = sb[0] + rb[0]
             cz.append(send(sb.at[1], rb.at[1], xn))
         elif n == 1:
@@ -460,24 +510,24 @@
                 to = lax.rem(z + k, nz)
                 cz.append(send(sb.at[3], rz.at[z], at(g, to, x, core)))
 
-    stages = (stage1, stage2, stage3, stage4)
-    lag = (0, 2, 3, 5)
-    for step in range(PAIRS + lag[-1]):
-        for stage, behind in zip(stages, lag):
-            q = step - behind
-            if 0 <= q < PAIRS:
-                stage(2 * q)
-                stage(2 * q + 1)
-        small(step - 1)
+    for stage, q in PLAN:
+        if stage == 0:
+            if q == 0:
+                small_terms()
+                cz.append(send(sb.at[0], rb.at[0], partner))
+            else:
+                small(q - 1)
+        else:
+            (stage1, stage2, stage3, stage4)[stage - 1](q)
     for cp in cz:
         cp.wait_recv()
     total = rz[0]
     for k in range(1, nz):
         total = total + rz[k]
     small_ref[...] = total
-    for p in range(parts):
-        h4[p].wait_recv()
-        out_ref[pl.ds(pl.multiple_of((1 - g) * half_rows, half_rows), half_rows), pl.ds(p * pw, pw)] = r4[p]
+    for q in range(PAIRS):
+        h4[q].wait_recv()
+        out_ref[pl.ds(pl.multiple_of((1 - g) * half_rows, half_rows), half_rows), pl.ds(2 * q * pw, 2 * pw)] = r4[q]
     for cp in sends:
         cp.wait_send()
 
@@ -517,7 +567,7 @@
     parts = 2 * PAIRS
     pw = width_s // parts
     slots = 4 * nz
-    f32, bf16 = jnp.float32, jnp.bfloat16
+    f32, bf16, i16 = jnp.float32, jnp.bfloat16, jnp.int16
     vm = pltpu.VMEM
     split = lambda v: v.reshape(-1, 1, LANES)
     anyspec = pl.BlockSpec(memory_space=pl.ANY)
@@ -545,14 +595,18 @@
             vm((2 * rp, LANES), f32),
             vm((width_s // 2, 2 * row_count), bf16),
             vm((2 * row_count, width_s), bf16),
+            vm((2 * row_count, LANES), f32),
             vm((parts, 2, 2, nz, half_rows, pw), f32),
+            vm((parts, 2 * nz * half_rows + CODE_ROWS, pw), i16),
+            vm((parts, 2 * nz * half_rows + CODE_ROWS, pw), i16),
             vm((parts, 2, nz, half_rows, pw), f32),
-            vm((parts, 2, nz, half_rows, pw), f32),
+            vm((parts, nz * half_rows + CODE_ROWS, pw), i16),
+            vm((parts, nz * half_rows + CODE_ROWS, pw), i16),
             vm((parts, nz, half_rows, pw), f32),
-            vm((parts, nz, half_rows, pw), f32),
-            vm((parts, nz - 1, half_rows, pw), f32),
-            vm((parts, half_rows, pw), f32),
-            vm((parts, half_rows, pw), f32),
+            vm((PAIRS, nz, 2 * half_rows + CODE_ROWS, pw), i16),
+            vm((PAIRS, nz - 1, 2 * half_rows + CODE_ROWS, pw), i16),
+            vm((PAIRS, half_rows, 2 * pw), f32),
+            vm((PAIRS, half_rows, 2 * pw), f32),
             vm((4, 8, width_s), f32),
             vm((3, 8, width_s), f32),
             vm((nz, 8, width_s), f32),
@@ -587,7 +641,7 @@
         and units == devices * LANES
         and (rows // devices) % LANES == 0
         and (2 * width_s // fsdp_count) % LANES == 0
-        and width_s % (2 * PAIRS * LANES) == 0
+        and width_s == 2 * PAIRS * LANES
     )
 
 

time: 115 us -> 109 us (0.948)
  Pallas kernels: 110 us -> 104 us
    pallas_call x1, Pallas kernels: 110 us -> 104 us  [shards_fused(): pl.pallas_call(functools.partial(fused, fsdp_count, rp), out_shape=(jax.S...]
where the time goes in v3:
time: 109 us
  Pallas kernels  104 us (95%)
  local copies, waits for them, and re-layouts  3.11 us (3%)
  between operations  1.29 us (1%)
    pallas_call x1, Pallas kernels, shards_fused(): pl.pallas_call(functools.partial(fused, fsdp_count, rp), out_shape=(jax.S...  104 us

profile of v3, /device:TPU:0, one launch (start us, length us, event | category | flops | bytes accessed | tf_op | source)
XLA Modules:
  0.0 108.6 jit_solution(7412629238006968378)
XLA Ops:
  1.3 0.6 fusion.live_ref
  1.9 103.6 %shard_map.121 = (f32[64,1024]{1,0:T(8,128)}, f32[8,1024]{1,0:T(8,128)}) custom-call(bf16[640,2048]{1,0:T(8,128)(2,1)} %t_ref.1, bf16[640,1024]{1,0:T(8,128)(2,1)} %s_ref.1, f32[5,128]{1,0:T(8,128)} %fusion.live_ref, bf16[2048,128]{1,0:T(8,128)(2,1)} %w_ref.1, f32[32,1,128]{2,1,0:T(1,128)} %bitcast.9, f32[32,1,128]{2,1,0:T(1,128)} %bitcast.10, ...), custom_call_target="tpu_custom_call" | custom-call | tf_op jit(solution)/shard_map/pallas_call | solution.py:575
  105.5 1.4 %fusion.1 = (f32[1,1024]{1,0:T(1,128)}, f32[1,1024]{1,0:T(1,128)}) fusion(f32[8,1024]{1,0:T(8,128)} %get-tuple-element.6), kind=kLoop, calls=%fused_computation.2 | loop fusion | bytes 16384 | tf_op jit(solution)/shard_map/slice | solution.py:625
  106.9 1.7 %copy.15 = f32[64,1024]{1,0:T(8,128)} copy(f32[64,1024]{1,0:T(8,128)} %get-tuple-element.12) | data formatting | bytes 524288

commit v4 on v3

--- a/solution.py
+++ b/solution.py
@@ -70,9 +70,9 @@
 )
 
 
-def fused(fsdp_count, rp, t_ref, s_ref, live_ref, w_ref, bias_ref, gain_ref, head_ref, cw_ref, cb_ref, ow_ref,
+def fused(fsdp_count, rp, loss_scale, t_ref, s_ref, count_ref, w_ref, bias_ref, gain_ref, head_ref, cw_ref, cb_ref, ow_ref,
           out_ref, small_ref,
-          wbuf, rows, xs, cw, pre, ssq, gains, heads, mixed, msg1, in1, msg2, in2, rr, er, xt, dbuf,
+          wbuf, rows, xs, cw, pre, ssq, heads, mixed, msg1, in1, msg2, in2, rr, er, xt, dbuf,
           ecol, tw, q1, r1, s1, q2, r2, tt, q3, r3, fin, r4, sb, rb, rz, lsem, ssem, rsem, wsem):
     g = lax.axis_index("group")
     f = lax.axis_index("fsdp")
@@ -207,7 +207,8 @@
     ssq[...] = jnp.zeros_like(ssq)
     for ref in (msg1, msg2, er, rr):
         ref[...] = jnp.zeros_like(ref)
-    msg1[pl.ds(3 * rp, rt), :] = live_ref[...]
+    row = lax.broadcasted_iota(jnp.int32, (rt, LANES), 0) * LANES + lax.broadcasted_iota(jnp.int32, (rt, LANES), 1)
+    msg1[pl.ds(3 * rp, rt), :] = jnp.where(row < count_ref[0], loss_scale, 0.0)
 
     locals_[0].wait()
     locals_[1].wait()
@@ -228,20 +229,26 @@
 
     mt = row_count
 
-    def project(dx, dy, n):
-        s = slot(dx, dy, n)
+    def column_block(dx, dy, n):
         y_ = g if dy == 0 else 1 - g
         x_ = x if dx == 0 else 1 - x
-        index = y_ * fsdp_count + (plane[n] * 2 + x_) * 2 + core
-        gains[pl.ds(s, 1), :] = gain_ref[index] * 0.5
-        heads[pl.ds(s, 1), :] = head_ref[index]
-        bias = bias_ref[index]
+        return y_ * fsdp_count + (plane[n] * 2 + x_) * 2 + core
+
+    def project(*blocks):
+        found = []
+        for b_ in blocks:
+            index = column_block(*b_)
+            heads[pl.ds(slot(*b_), 1), :] = head_ref[index]
+            found.append((slot(*b_), gain_ref[index] * 0.5, bias_ref[index]))
 
         def step(t, carry):
             ds = pl.ds(pl.multiple_of(t * mt, mt), mt)
-            p = jnp.dot(rows[ds, :], wbuf[s], preferred_element_type=jnp.float32) + bias
-            pre[s, ds, :] = p
-            ssq[ds, :] += p * p
+            w = jnp.concatenate([wbuf[s] for s, _, _ in found], axis=1) if len(found) > 1 else wbuf[found[0][0]]
+            both = jnp.dot(rows[ds, :], w, preferred_element_type=jnp.float32)
+            for i, (s, gain, bias) in enumerate(found):
+                p = both[:, i * LANES:(i + 1) * LANES] + bias
+                pre[s, ds, :] = p * gain
+                ssq[ds, :] += p * p
             return carry
 
         lax.fori_loop(0, 2 * row_count // mt, step, 0)
@@ -263,7 +270,7 @@
                 pass_on((0, 0, 1), (0, 0, 3), q, zmid, 'mid')
 
     rows_in.wait_recv()
-    project(0, 0, 0)
+    project((0, 0, 0))
 
     @pl.when(is_end)
     def _():
@@ -271,7 +278,7 @@
 
     sideways((0, 0, 1), 1)
     rest(0)
-    project(1, 0, 0)
+    project((1, 0, 0))
 
     def far(q):
         landed(0, 0, 3, [q])
@@ -281,7 +288,7 @@
     def _():
         far(0)
 
-    project(0, 1, 0)
+    project((0, 1, 0))
     for i, q in enumerate(order):
         landed(1, 1, 0, [q])
 
@@ -295,7 +302,7 @@
             if i == 1:
                 far(1)
 
-    project(0, 0, 1)
+    project((0, 0, 1))
     xs_in.wait_recv()
     pick = (
         lax.broadcasted_iota(jnp.int32, (block, 2 * block), 1)
@@ -303,9 +310,13 @@
     )
     pick = jnp.where(pick, 1.0, 0.0).astype(jnp.bfloat16)
     for j in range(fsdp_count // 2):
-        xt[pl.ds(j * block, block), :] = lax.dot_general(
+        turned = lax.dot_general(
             pick, xs[:, pl.ds(j * 2 * block, 2 * block)], (((1,), (1,)), ((), ())), preferred_element_type=jnp.float32
         ).astype(jnp.bfloat16)
+        far_x = lax.rem(x + j % 2, 2)
+        for y_ in range(2):
+            to = ((lax.rem(g + y_, 2) * 2 + far_x) * nz + j // 2) * half_rows
+            xt[pl.ds(pl.multiple_of(to, half_rows), half_rows), :] = turned[y_ * half_rows:(y_ + 1) * half_rows, :]
 
     @pl.when(is_mid)
     def _():
@@ -319,10 +330,10 @@
         landed(0, 0, 2, quarters)
 
     sideways((0, 0, 2), 2)
-    project(1, 1, 0)
-    project(0, 0, 2)
+    project((1, 1, 0))
+    project((0, 0, 2))
     landed(1, 0, 1, quarters)
-    project(1, 0, 1)
+    project((1, 0, 1))
     landed(0, 1, 1, quarters)
 
     @pl.when(is_end)
@@ -330,7 +341,7 @@
         landed(0, 0, 3, quarters)
 
     sideways((0, 0, 3), 3)
-    project(0, 1, 1)
+    project((0, 1, 1))
 
     @pl.when(is_mid)
     def _():
@@ -338,24 +349,23 @@
             landed(1, 1, 2, [q])
             pass_on((1, 1, 2), (1, 1, 2), q, zpair, 'mid')
 
-    project(0, 0, 3)
+    project((0, 0, 3))
     for at_ in ((1, 0, 2), (0, 1, 2)):
         landed(*at_, quarters)
-        project(*at_)
+        project(at_)
     diagonal(3)
     landed(1, 1, 1, quarters)
-    project(1, 1, 1)
+    project((1, 1, 1))
     rest(3)
-    project(1, 0, 3)
-    project(0, 1, 3)
+    project((1, 0, 3))
+    project((0, 1, 3))
 
     @pl.when(is_end)
     def _():
         landed(1, 1, 2, quarters)
 
-    project(1, 1, 2)
     landed(1, 1, 3, quarters)
-    project(1, 1, 3)
+    project((1, 1, 2), (1, 1, 3))
 
     for h in range(2):
         def squares(t, carry, h=h):
@@ -375,7 +385,7 @@
             r = to_col(rr[pl.ds(h * rp + t, 1), :])
             acc = jnp.zeros((LANES, LANES), jnp.float32)
             for s in range(4 * nz):
-                v = pre[s, tile(h * rt + t), :] * r * gains[pl.ds(s, 1), :]
+                v = pre[s, tile(h * rt + t), :] * r
                 acc += (v * jnp.tanh(v) + v) * heads[pl.ds(s, 1), :]
             msg2[pl.ds(h * rp + t, 1), :] = to_row(jnp.sum(acc, axis=1, keepdims=True))
             return carry
@@ -395,16 +405,17 @@
     lax.fori_loop(0, rt, spread, 0)
     sb[...] = jnp.zeros_like(sb)
 
-    def scale_cross(p):
-        cols = pl.ds(p * pw, pw)
+    def scale_cross(q):
+        cols = pl.ds(2 * q * pw, 2 * pw)
         owp = ow_ref[:, cols]
 
         def cross_tile(t, carry):
-            d = ecol[tile(t), :] * owp * xs[tile(t), cols].astype(jnp.float32)
+            e = ecol[tile(t), :]
+            d = jnp.concatenate([e, e], axis=1) * owp * xs[tile(t), cols].astype(jnp.float32)
             dbuf[tile(t), cols] = d.astype(jnp.bfloat16)
             return carry
 
-        lax.fori_loop(0, 2 * rt, cross_tile, 0)
+        lax.fori_loop(0, 2 * rt, cross_tile, 0, unroll=2)
 
     def small_terms():
         def one(t, carry):
@@ -440,39 +451,37 @@
         return out
 
     def way(p):
-        return (g, x, yn, xn) if p % 2 == 0 else (x, g, xn, yn)
+        return (yn, xn) if p % 2 == 0 else (xn, yn)
 
     h1, h2, h3, h4 = {}, {}, {}, {}
+    side = nz * half_rows
 
     def stage1(q):
+        scale_cross(q)
+        val = jnp.dot(xt[...], dbuf[:, pl.ds(2 * q * pw, 2 * pw)], preferred_element_type=jnp.float32)
         for p in (2 * q, 2 * q + 1):
-            scale_cross(p)
-            val = jnp.dot(xt[...], dbuf[:, pl.ds(p * pw, pw)], preferred_element_type=jnp.float32)
-            for z_ in range(nz):
-                for x_ in range(2):
-                    for y_ in range(2):
-                        first, second = (y_, x_) if p % 2 == 0 else (x_, y_)
-                        offset = ((z_ * 2 + x_) * 2 + y_) * half_rows
-                        tw[p, first, second, z_] = val[offset:offset + half_rows, :]
-            first, second, n1, n2 = way(p)
-            encode([tw[p, 1 - first, s_, z_] for s_ in range(2) for z_ in range(nz)], q1.at[p])
-            h1[p] = send(q1.at[p], r1.at[p], n1)
+            v = val[:, (p % 2) * pw:(p % 2 + 1) * pw]
+            keep, give = ((0, 1), (2, 3)) if p % 2 == 0 else ((0, 2), (1, 3))
+            out = [v[c * side + z_ * half_rows:c * side + (z_ + 1) * half_rows, :] for c in give for z_ in range(nz)]
+            encode(out, q1.at[p])
+            h1[p] = send(q1.at[p], r1.at[p], way(p)[0])
+            for i, c in enumerate(keep):
+                tw[p, i] = v[c * side:(c + 1) * side, :]
 
     def stage2(q):
         for p in (2 * q, 2 * q + 1):
-            first, second, n1, n2 = way(p)
             h1[p].wait_recv()
-            for i, v in enumerate(decode(r1.at[p], 2 * nz)):
-                s1[p, i // nz, i % nz] = tw[p, first, i // nz, i % nz] + v
-            encode([s1[p, 1 - second, z_] for z_ in range(nz)], q2.at[p])
-            h2[p] = send(q2.at[p], r2.at[p], n2)
+            got = decode(r1.at[p], 2 * nz)
+            encode([tw[p, 1, pl.ds(z_ * half_rows, half_rows), :] + got[nz + z_] for z_ in range(nz)], q2.at[p])
+            h2[p] = send(q2.at[p], r2.at[p], way(p)[1])
+            for z_ in range(nz):
+                s1[p, z_] = tw[p, 0, pl.ds(z_ * half_rows, half_rows), :] + got[z_]
 
     def stage3(q):
         for p in (2 * q, 2 * q + 1):
-            first, second, n1, n2 = way(p)
             h2[p].wait_recv()
             for z_, v in enumerate(decode(r2.at[p], nz)):
-                tt[p, z_] = s1[p, second, z_] + v
+                tt[p, z_] = s1[p, z_] + v
         for z_ in range(nz):
             encode([tt[2 * q, z_], tt[2 * q + 1, z_]], q3.at[q, z_])
         h3[q] = []
@@ -558,7 +567,6 @@
     group_count = lax.axis_size("group")
     fsdp_count = lax.axis_size("fsdp")
     loss_scale = math.sqrt(width_s / (row_count * group_count * fsdp_count))
-    live = (jnp.arange(row_count, dtype=jnp.int32) < counts[0]).astype(jnp.float32) * loss_scale
     rt = row_count // LANES
     rp = -(-rt // 8) * 8
     nz = fsdp_count // 4
@@ -573,9 +581,9 @@
     anyspec = pl.BlockSpec(memory_space=pl.ANY)
     vspec = pl.BlockSpec(memory_space=pltpu.VMEM)
     grad, small = pl.pallas_call(
-        functools.partial(fused, fsdp_count, rp),
+        functools.partial(fused, fsdp_count, rp, loss_scale),
         out_shape=(jax.ShapeDtypeStruct((block, width_s), f32), jax.ShapeDtypeStruct((8, width_s), f32)),
-        in_specs=[anyspec, anyspec, vspec, anyspec, vspec, vspec, vspec, anyspec, vspec, vspec],
+        in_specs=[anyspec, anyspec, pl.BlockSpec(memory_space=pltpu.SMEM), anyspec, vspec, vspec, vspec, anyspec, vspec, vspec],
         out_specs=(vspec, vspec),
         scratch_shapes=[
             vm((slots, fin_width, LANES), bf16),
@@ -584,7 +592,6 @@
             vm((width_s, width_s), bf16),
             vm((slots, 2 * row_count, LANES), f32),
             vm((2 * row_count, LANES), f32),
-            vm((slots, LANES), f32),
             vm((slots, LANES), f32),
             vm((row_count, width_s), f32),
             vm((4 * rp, LANES), f32),
@@ -596,10 +603,10 @@
             vm((width_s // 2, 2 * row_count), bf16),
             vm((2 * row_count, width_s), bf16),
             vm((2 * row_count, LANES), f32),
-            vm((parts, 2, 2, nz, half_rows, pw), f32),
+            vm((parts, 2, nz * half_rows, pw), f32),
             vm((parts, 2 * nz * half_rows + CODE_ROWS, pw), i16),
             vm((parts, 2 * nz * half_rows + CODE_ROWS, pw), i16),
-            vm((parts, 2, nz, half_rows, pw), f32),
+            vm((parts, nz, half_rows, pw), f32),
             vm((parts, nz * half_rows + CODE_ROWS, pw), i16),
             vm((parts, nz * half_rows + CODE_ROWS, pw), i16),
             vm((parts, nz, half_rows, pw), f32),
@@ -619,7 +626,7 @@
             collective_id=0, has_side_effects=True, vmem_limit_bytes=60 * 1024 * 1024
         ),
     )(
-        teacher_rows, student_rows, live.reshape(rt, LANES), teacher_weight, split(teacher_bias), split(teacher_gain),
+        teacher_rows, student_rows, counts, teacher_weight, split(teacher_bias), split(teacher_gain),
         split(teacher_head), cross_weight, cross_bias[None, :], out_weight[None, :],
     )
     return (grad, small[0], small[1])

time: 109 us -> 104 us (0.954)
  Pallas kernels: 104 us -> 99.7 us
    pallas_call x1, Pallas kernels: 104 us -> 99.7 us  [shards_fused(): pl.pallas_call(functools.partial(fused, fsdp_count, rp, loss_scale), out_...]
where the time goes in v4:
time: 104 us
  Pallas kernels  99.7 us (96%)
  local copies, waits for them, and re-layouts  3.11 us (3%)
  between operations  1.29 us (1%)
    pallas_call x1, Pallas kernels, shards_fused(): pl.pallas_call(functools.partial(fused, fsdp_count, rp, loss_scale), out_...  99.7 us

profile of v4, /device:TPU:0, one launch (start us, length us, event | category | flops | bytes accessed | tf_op | source)
XLA Modules:
  0.0 104.1 jit_solution(16435220743840316865)
XLA Ops:
  1.3 99.7 %shard_map.121 = (f32[64,1024]{1,0:T(8,128)}, f32[8,1024]{1,0:T(8,128)}) custom-call(bf16[640,2048]{1,0:T(8,128)(2,1)} %t_ref.1, bf16[640,1024]{1,0:T(8,128)(2,1)} %s_ref.1, s32[1]{0:T(128)S(6)} %copy.14.count_ref, bf16[2048,128]{1,0:T(8,128)(2,1)} %w_ref.1, f32[32,1,128]{2,1,0:T(1,128)} %bitcast.7, f32[32,1,128]{2,1,0:T(1,128)} %bitcast.8, ...), custom_call_target="tpu_custom_call" | custom-call | tf_op jit(solution)/shard_map/pallas_call | solution.py:583
  101.0 1.4 %fusion = (f32[1,1024]{1,0:T(1,128)}, f32[1,1024]{1,0:T(1,128)}) fusion(f32[8,1024]{1,0:T(8,128)} %get-tuple-element.6), kind=kLoop, calls=%fused_computation | loop fusion | bytes 16384 | tf_op jit(solution)/shard_map/slice | solution.py:632
  102.4 1.7 %copy.15 = f32[64,1024]{1,0:T(8,128)} copy(f32[64,1024]{1,0:T(8,128)} %get-tuple-element.12) | data formatting | bytes 524288

commit v5 on v4

--- a/solution.py
+++ b/solution.py
@@ -65,7 +65,7 @@
 CODE_BITS = 15.0
 CODE_MOST = 32767.0
 PLAN = (
-    (1, 0), (1, 1), (0, 0), (1, 2), (2, 0), (1, 3), (0, 1), (2, 1), (3, 0), (0, 2), (2, 2), (3, 1), (2, 3), (0, 3), (3, 2), (4, 0),
+    (1, 0), (1, 1), (1, 2), (2, 0), (1, 3), (0, 0), (2, 1), (3, 0), (0, 1), (2, 2), (3, 1), (0, 2), (2, 3), (3, 2), (4, 0), (0, 3),
     (3, 3), (4, 1), (4, 2), (4, 3),
 )
 
@@ -373,7 +373,7 @@
             msg1[pl.ds(h * rp + t, 1), :] = to_row(col)
             return carry
 
-        lax.fori_loop(0, rt, squares, 0)
+        lax.fori_loop(0, rt, squares, 0, unroll=True)
     m1 = send(msg1, in1, partner)
     m1.wait_recv()
     for h in range(2):
@@ -402,7 +402,7 @@
         ecol[tile(rt + t), :] = jnp.broadcast_to(to_col(er[pl.ds(rp + t, 1), :]), (LANES, LANES))
         return carry
 
-    lax.fori_loop(0, rt, spread, 0)
+    lax.fori_loop(0, rt, spread, 0, unroll=True)
     sb[...] = jnp.zeros_like(sb)
 
     def scale_cross(q):

time: 104 us -> 103 us (level)
  Pallas kernels: 99.7 us -> 98.4 us
    pallas_call x1, Pallas kernels: 99.7 us -> 98.4 us  [shards_fused(): pl.pallas_call(functools.partial(fused, fsdp_count, rp, loss_scale), out_...]
where the time goes in v5:
time: 103 us
  Pallas kernels  98.4 us (96%)
  local copies, waits for them, and re-layouts  3.11 us (3%)
  between operations  1.29 us (1%)
    pallas_call x1, Pallas kernels, shards_fused(): pl.pallas_call(functools.partial(fused, fsdp_count, rp, loss_scale), out_...  98.4 us

profile of v5, /device:TPU:0, one launch (start us, length us, event | category | flops | bytes accessed | tf_op | source)
XLA Modules:
  0.0 102.8 jit_solution(8717732523466817292)
XLA Ops:
  1.3 98.4 %shard_map.121 = (f32[64,1024]{1,0:T(8,128)}, f32[8,1024]{1,0:T(8,128)}) custom-call(bf16[640,2048]{1,0:T(8,128)(2,1)} %t_ref.1, bf16[640,1024]{1,0:T(8,128)(2,1)} %s_ref.1, s32[1]{0:T(128)S(6)} %copy.14.count_ref, bf16[2048,128]{1,0:T(8,128)(2,1)} %w_ref.1, f32[32,1,128]{2,1,0:T(1,128)} %bitcast.7, f32[32,1,128]{2,1,0:T(1,128)} %bitcast.8, ...), custom_call_target="tpu_custom_call" | custom-call | tf_op jit(solution)/shard_map/pallas_call | solution.py:583
  99.7 1.4 %fusion = (f32[1,1024]{1,0:T(1,128)}, f32[1,1024]{1,0:T(1,128)}) fusion(f32[8,1024]{1,0:T(8,128)} %get-tuple-element.6), kind=kLoop, calls=%fused_computation | loop fusion | bytes 16384 | tf_op jit(solution)/shard_map/slice | solution.py:632
  101.1 1.7 %copy.15 = f32[64,1024]{1,0:T(8,128)} copy(f32[64,1024]{1,0:T(8,128)} %get-tuple-element.12) | data formatting | bytes 524288
